TPU v7x, 32 devices: a whole 2x2x4 slice. The times are simulated.
32 devices in a mesh: band: 8 (over z, y), grid: 4 (over x, core).
Axes of the slice: x: 2, y: 2, z: 4, core: 2. Of those that a mesh axis runs over, the one named last changes fastest.
Arguments:
- bands: bfloat16 [2, 16, 128, 128, 128], P(None, 'band', 'grid'), may hold values from -6 to 6
- occupations: float32 [16], P('band'), may hold values from 0.25 to 1
- external: float32 [128, 128, 128], P('grid'), may hold values from 0 to 2
- density_in: float32 [128, 128, 128], P('grid'), may hold values from -0.2 to 1.4
- prev_density: float32 [128, 128, 128], P('grid'), may hold values from 0 to 1.2
- prev_residual: float32 [128, 128, 128], P('grid'), may hold values from -1.3 to 0.3
- hist_density: float32 [5, 128, 128, 128], P(None, 'grid'), may hold values from 0 to 1
- hist_residual: float32 [5, 128, 128, 128], P(None, 'grid'), may hold values from -0.6 to 1
Outputs:
- density: float32 [128, 128, 128], P('grid')
- residual: float32 [128, 128, 128], P('grid')
All inputs are finite; a program needn't handle non-finite values.
Results may differ from a plain program's by a relative error of at most 0.018.
The roundings to bfloat16 on the way count: a program that leaves them out, or rounds other values in their place, can miss the bound.
Values may be sent and summed in bfloat16 or wider, within the bound.
No kernel may reach another device: no remote copies, remote signals or barrier semaphores. Data moves between devices by JAX's collectives and lax.ppermute only.
A program may use at most 192 MiB of HBM per device.

v0:
```python
import math
import jax
import jax.numpy as jnp
from jax import lax
from jax.sharding import PartitionSpec as P

NG = 128
DEPTH = 6
ITERS = 3
time_step = 0.25
energy_shift = 2.5
coupling = 1.0
mixing_weight = 0.5
ridge_share = 0.1
ridge_floor = 0.01
density_scale = 8.0
highest = lax.Precision.HIGHEST


def fourier_tables(length, frequency):
    positions = jnp.arange(length, dtype=jnp.int32)
    phase_index = positions[:, None] * frequency[None, :] % length
    angles = phase_index.astype(jnp.float32) * (2.0 * math.pi / length)
    unit_scale = 1.0 / math.sqrt(length)
    return (
        (jnp.cos(angles) * unit_scale).astype(jnp.bfloat16),
        (jnp.sin(angles) * unit_scale).astype(jnp.bfloat16),
    )


def complex_block(cosine_part, sine_part, orientation):
    sine_signed = sine_part * orientation
    upper_half = jnp.concatenate([cosine_part, sine_signed], axis=1)
    lower_half = jnp.concatenate([-sine_signed, cosine_part], axis=1)
    return jnp.concatenate([upper_half, lower_half], axis=0)


def solve_definite(matrix, vector):
    extent = matrix.shape[0]
    factor_low = jnp.zeros_like(matrix)
    for column in range(extent):
        pivot_value = jnp.sqrt(
            matrix[column, column]
            - jnp.sum(factor_low[column, :column] * factor_low[column, :column])
        )
        factor_low = factor_low.at[column, column].set(pivot_value)
        for row_index in range(column + 1, extent):
            element = (
                matrix[row_index, column]
                - jnp.sum(factor_low[row_index, :column] * factor_low[column, :column])
            ) / pivot_value
            factor_low = factor_low.at[row_index, column].set(element)
    middle = jnp.zeros_like(vector)
    for row_index in range(extent):
        element = (
            vector[row_index] - jnp.sum(factor_low[row_index, :row_index] * middle[:row_index])
        ) / factor_low[row_index, row_index]
        middle = middle.at[row_index].set(element)
    result = jnp.zeros_like(vector)
    for row_index in reversed(range(extent)):
        element = (
            middle[row_index]
            - jnp.sum(factor_low[row_index + 1 :, row_index] * result[row_index + 1 :])
        ) / factor_low[row_index, row_index]
        result = result.at[row_index].set(element)
    return result


def local(
    bands,
    occupations,
    external,
    density_in,
    prev_density,
    prev_residual,
    hist_density,
    hist_residual,
):
    grid_count = lax.axis_size("grid")
    band_count = lax.axis_size("band")
    slab_planes = external.shape[0]
    cells_total = NG * NG * NG
    bands_total = occupations.shape[0] * band_count
    frequency = jnp.arange(-(NG // 4), NG // 4, dtype=jnp.int32)
    kept_count = frequency.shape[0]
    inside = ((frequency >= -(NG // 4)) & (frequency < NG // 4)).astype(jnp.float32)
    cosine_part, sine_part = fourier_tables(NG, frequency)
    forward_block = complex_block(cosine_part, sine_part, -1.0)
    inverse_block = complex_block(cosine_part.T, sine_part.T, 1.0)
    forward_axis = forward_block.reshape(2, NG, 2, kept_count)
    inverse_axis = inverse_block.reshape(2, kept_count, 2, NG)
    column_rows = kept_count // grid_count
    column_start = lax.axis_index("grid") * column_rows
    local_freq = lax.dynamic_slice_in_dim(frequency, column_start, column_rows).astype(jnp.float32)
    local_inside = lax.dynamic_slice_in_dim(inside, column_start, column_rows)
    squared = frequency.astype(jnp.float32) * frequency.astype(jnp.float32)
    quarter = NG / 4.0
    radius = (
        squared[None, :, None] + (local_freq * local_freq)[:, None, None] + squared[None, None, :]
    )
    kinetic = jnp.exp(-time_step * radius / (quarter * quarter))
    kinetic = kinetic * local_inside[:, None, None] * inside[None, :, None] * inside[None, None, :]
    history_flat = hist_residual.reshape(DEPTH - 1, -1)
    gram_kept = lax.psum(
        jnp.dot(history_flat, history_flat.T, precision=highest) / cells_total, "grid"
    )
    orbitals = jnp.concatenate([bands[0], bands[1]], axis=-1)
    density_now = density_in
    density_prev = prev_density
    residual_prev = prev_residual
    density_diffs = hist_density
    residual_diffs = hist_residual
    residual = density_in
    for iteration in range(ITERS):
        factor = jnp.exp(-time_step * (external + coupling * density_now - energy_shift))
        doubled = jnp.concatenate([factor, factor], axis=-1)
        weighted = (orbitals.astype(jnp.float32) * doubled).astype(jnp.bfloat16)
        band_items = orbitals.shape[0]
        along_z = jnp.dot(weighted, forward_block, preferred_element_type=jnp.float32).astype(
            jnp.bfloat16
        )
        split_z = along_z.reshape(band_items, slab_planes, NG, 2, kept_count)
        along_y = jnp.einsum(
            "bxycz,cydk->bkxdz", split_z, forward_axis, preferred_element_type=jnp.float32
        )
        along_y = along_y.astype(jnp.bfloat16).reshape(
            band_items, kept_count, slab_planes, 2 * kept_count
        )
        exchanged = lax.all_to_all(along_y, "grid", split_axis=1, concat_axis=2, tiled=True)
        item_count = exchanged.shape[0]
        spread = exchanged.reshape(item_count, column_rows, NG, 2, kept_count)
        spectral = jnp.einsum(
            "byxcz,cxdk->bykdz", spread, forward_axis, preferred_element_type=jnp.float32
        )
        damped = (spectral * kinetic[None, :, :, None, :]).astype(jnp.bfloat16)
        spatial = jnp.einsum(
            "bykdz,dkcx->byxcz", damped, inverse_axis, preferred_element_type=jnp.float32
        )
        returned = lax.all_to_all(
            spatial.astype(jnp.bfloat16).reshape(item_count, column_rows, NG, 2 * kept_count),
            "grid",
            split_axis=2,
            concat_axis=1,
            tiled=True,
        )
        split_back = returned.reshape(band_items, kept_count, slab_planes, 2, kept_count)
        back_y = jnp.einsum(
            "bkxdz,dkcy->bxycz", split_back, inverse_axis, preferred_element_type=jnp.float32
        )
        back_y = back_y.astype(jnp.bfloat16).reshape(band_items, slab_planes, NG, 2 * kept_count)
        orbitals = jnp.dot(back_y, inverse_block, preferred_element_type=jnp.float32).astype(
            jnp.bfloat16
        )
        real_part = orbitals[..., :NG].astype(jnp.float32)
        imag_part = orbitals[..., NG:].astype(jnp.float32)
        weighted_sq = occupations[:, None, None, None] * (
            real_part * real_part + imag_part * imag_part
        )
        density_out = lax.psum(
            (jnp.sum(weighted_sq, axis=0) * (density_scale / bands_total)).astype(jnp.bfloat16),
            "band",
        ).astype(jnp.float32)
        mixing_density_diffs = density_diffs
        mixing_residual_diffs = residual_diffs
        mixing_residual = density_out - density_now
        newest = mixing_residual - residual_prev
        mixing_density_diffs = jnp.concatenate(
            [
                mixing_density_diffs[mixing_density_diffs.shape[0] - (DEPTH - 1) :],
                (density_now - density_prev)[None],
            ],
            axis=0,
        )
        mixing_residual_diffs = jnp.concatenate(
            [mixing_residual_diffs[mixing_residual_diffs.shape[0] - (DEPTH - 1) :], newest[None]],
            axis=0,
        )
        flat_diffs = mixing_residual_diffs.reshape(DEPTH, -1)
        border_local = jnp.dot(flat_diffs, newest.reshape(-1), precision=highest) / cells_total
        right_local = (
            jnp.dot(flat_diffs, mixing_residual.reshape(-1), precision=highest) / cells_total
        )
        border, right_side = lax.psum((border_local, right_local), "grid")
        gram_matrix = (
            jnp.zeros((DEPTH, DEPTH), jnp.float32).at[: DEPTH - 1, : DEPTH - 1].set(gram_kept)
        )
        gram_matrix = gram_matrix.at[DEPTH - 1, :].set(border).at[:, DEPTH - 1].set(border)
        ridge_value = ridge_share * jnp.trace(gram_matrix) / DEPTH + ridge_floor
        coeffs = solve_definite(
            gram_matrix + ridge_value * jnp.eye(DEPTH, dtype=jnp.float32), right_side
        )
        combined = mixing_density_diffs + mixing_weight * mixing_residual_diffs
        density_next = (
            density_now
            + mixing_weight * mixing_residual
            - jnp.einsum("j,jxyz->xyz", coeffs, combined, precision=highest)
        )
        density_next, residual, density_diffs, residual_diffs, gram_kept = (
            density_next,
            mixing_residual,
            mixing_density_diffs,
            mixing_residual_diffs,
            gram_matrix[1:, 1:],
        )
        density_prev = density_now
        residual_prev = residual
        density_now = density_next
    return (density_now, residual)


def solution(mesh):
    placed = (
        P(None, "band", "grid", None, None),
        P("band"),
        P("grid", None, None),
        P("grid", None, None),
        P("grid", None, None),
        P("grid", None, None),
        P(None, "grid", None, None),
        P(None, "grid", None, None),
    )
    return jax.shard_map(
        local,
        mesh=mesh,
        in_specs=placed,
        out_specs=(P("grid", None, None), P("grid", None, None)),
        check_vma=False,
    )
```

profile of v0, /device:TPU:0, one launch (start us, length us, event | category | flops | bytes accessed | tf_op | source)
XLA Modules:
  0.0 1105.6 jit_solution(15028615402567349357)
XLA Ops:
  7.6 4.1 slice_bitcast_fusion.1
  14.5 4.4 fusion.49
  24.1 4.2 all-to-all-start
  29.3 13.4 %all-to-all-done = bf16[2,64,32,128]{3,2,0,1:T(8,128)(2,1)S(1)} async-done(((bf16[2,64,32,128]{3,2,0,1:T(8,128)(2,1)}), bf16[2,64,32,128]{3,2,0,1:T(8,128)(2,1)S(1)}, u32[]{:S(2)}, u32[]{:S(2)}) %all-to-all-start) | async-done | bytes 1048608 | tf_op jit(solution)/shard_map/all_to_all | solution.py:129
  43.9 3.9 reshape.2819
  51.8 28.3 %all_to_all.90 = bf16[2,16,128,128]{3,1,0,2:T(8,128)(2,1)S(1)} all-to-all(bf16[2,16,128,128]{3,1,0,2:T(8,128)(2,1)S(1)} %copy.65), channel_id=1, replica_groups=mesh['band'=8,'grid'=4] {'grid'}, dimensions={2} | all-to-all | bytes 2097152 | tf_op jit(solution)/shard_map/all_to_all | solution.py:139
  81.5 3.9 reshape.2821
  85.4 4.3 copy.69
  96.8 54.3 %fusion.83 = f32[5,5]{1,0:T(8,128)S(1)} fusion(f32[5,32,128,128]{3,2,1,0:T(8,128)} %param.231), kind=kOutput, calls=%fused_computation.118 | convolution fusion | flops 157286432 | bytes 10485860 | tf_op jit(solution)/shard_map/dot_general | solution.py:105
  151.1 25.1 %all-reduce.19.cloned.1.call-done = bf16[32,128,128]{2,1,0:T(8,128)(2,1)} async-done(((bf16[32,128,128]{2,1,0:T(8,128)(2,1)}), bf16[32,128,128]{2,1,0:T(8,128)(2,1)}) %all-reduce.19.cloned.1.call-update) | async-done | bytes 1048592 | tf_op jit(solution)/shard_map/psum | solution.py:159
  176.2 3.9 fusion.188
  180.1 13.4 %pad_maximum_fusion = (f32[6,32,128,128]{3,2,1,0:T(8,128)S(1)}, f32[6,32,128,128]{3,2,1,0:T(8,128)}) fusion(f32[1,32,128,128]{3,2,1,0:T(8,128)S(1)} %bitcast.527, f32[5,32,128,128]{3,2,1,0:T(8,128)} %param.231, f32[1,32,128,128]{3,2,1,0:T(8,128)S(1)} %get-tuple-element.1331, f32[5,32,128,128]{3,2,1,0:T(8,128)} %param.230), kind=kLoop, calls=%fused_computation.13 | loop fusion | flops 12582912 | bytes 50331648 | tf_op jit(solution)/shard_map/concatenate | solution.py:174
  193.5 43.1 %fusion.119 = f32[6]{0:T(128)S(1)} fusion(f32[32,128,128,1]{2,3,1,0:T(1,128)S(1)} %bitcast.531, f32[6,32,128,128]{3,2,1,0:T(8,128)S(1)} %get-tuple-element.1325), kind=kOutput, calls=%fused_computation.130 | convolution fusion | flops 37748744 | bytes 14680088 | tf_op jit(solution)/shard_map/dot_general | solution.py:181
  236.6 42.8 %fusion.116 = f32[6]{0:T(128)S(1)} fusion(f32[32,128,128,1]{2,3,1,0:T(1,128)S(1)} %bitcast.528, f32[6,32,128,128]{3,2,1,0:T(8,128)S(1)} %get-tuple-element.1325), kind=kOutput, calls=%fused_computation.129 | convolution fusion | flops 37748744 | bytes 14680088 | tf_op jit(solution)/shard_map/dot_general | solution.py:179
  279.5 6.9 all-reduce.14
  353.1 28.1 %fusion.16 = f32[1,32,128,128]{3,0,2,1:T(1,128)S(1)} fusion(f32[6,32,128,128]{3,2,1,0:T(8,128)} %get-tuple-element.1326, f32[6]{0:T(128)S(1)} %constant_dynamic-update-slice_fusion.26), kind=kOutput, calls=%fused_computation.24 | convolution fusion | flops 37748736 | bytes 14680088 | tf_op jit(solution)/shard_map/j,jxyz->xyz/dot_general | solution.py:196
  388.6 3.5 copy.190
  392.1 4.7 reshape.2947
  396.9 17.9 %all_to_all.91 = bf16[2,64,32,128]{3,2,0,1:T(8,128)(2,1)S(1)} all-to-all(bf16[2,64,32,128]{3,2,0,1:T(8,128)(2,1)} %reshape.2947), channel_id=1, replica_groups=mesh['band'=8,'grid'=4] {'grid'}, dimensions={1} | all-to-all | bytes 2097152 | tf_op jit(solution)/shard_map/all_to_all | solution.py:129
  415.9 5.0 reshape.2843
  420.9 3.4 fusion.78
  426.6 2.7 copy.84
  429.2 18.1 %all_to_all.92 = bf16[2,16,128,128]{3,1,0,2:T(8,128)(2,1)S(1)} all-to-all(bf16[2,16,128,128]{3,1,0,2:T(8,128)(2,1)} %copy.84), channel_id=1, replica_groups=mesh['band'=8,'grid'=4] {'grid'}, dimensions={2} | all-to-all | bytes 2097152 | tf_op jit(solution)/shard_map/all_to_all | solution.py:139
  448.7 5.0 reshape.2845
  453.8 6.5 copy.88
  467.5 15.0 %fusion.24 = (f32[5,32,128,128]{3,2,1,0:T(8,128)}, f32[5,32,128,128]{3,2,1,0:T(8,128)}) fusion(f32[5,32,128,128]{3,2,1,0:T(8,128)} %param.230, f32[1,32,128,128]{3,2,1,0:T(8,128)} %copy-done.14, f32[1,32,128,128]{3,2,1,0:T(8,128)S(1)} %bitcast.529, f32[5,32,128,128]{3,2,1,0:T(8,128)} %param.231), kind=kLoop, calls=%fused_computation.38 | loop fusion | flops 5242880 | bytes 46137344 | tf_op jit(solution)/shard_map/concatenate | solution.py:167
  482.5 61.3 %all-reduce.21.cloned.1.call-done = bf16[32,128,128]{2,1,0:T(8,128)(2,1)} async-done(((bf16[32,128,128]{2,1,0:T(8,128)(2,1)}), bf16[32,128,128]{2,1,0:T(8,128)(2,1)}) %all-reduce.21.cloned.1.call-update) | async-done | bytes 1048592 | tf_op jit(solution)/shard_map/psum | solution.py:159
  543.8 4.0 fusion.187
  547.9 4.3 copy-done
  552.2 9.3 pad_maximum_fusion.2
  561.5 43.1 %fusion.113 = f32[6]{0:T(128)S(1)} fusion(f32[32,128,128,1]{2,3,1,0:T(1,128)S(1)} %bitcast.530, f32[6,32,128,128]{3,2,1,0:T(8,128)S(1)} %get-tuple-element.1323), kind=kOutput, calls=%fused_computation.128 | convolution fusion | flops 37748744 | bytes 14680088 | tf_op jit(solution)/shard_map/dot_general | solution.py:181
  604.6 42.9 %fusion.110 = f32[6]{0:T(128)S(1)} fusion(f32[32,128,128,1]{2,3,1,0:T(1,128)S(1)} %bitcast.533, f32[6,32,128,128]{3,2,1,0:T(8,128)S(1)} %get-tuple-element.1323), kind=kOutput, calls=%fused_computation.127 | convolution fusion | flops 37748744 | bytes 14680088 | tf_op jit(solution)/shard_map/dot_general | solution.py:179
  647.4 6.5 all-reduce.13
  721.3 28.1 %fusion.14 = f32[1,32,128,128]{3,0,2,1:T(1,128)S(1)} fusion(f32[6,32,128,128]{3,2,1,0:T(8,128)} %get-tuple-element.1324, f32[6]{0:T(128)S(1)} %constant_dynamic-update-slice_fusion.25), kind=kOutput, calls=%fused_computation.22 | convolution fusion | flops 37748736 | bytes 14680088 | tf_op jit(solution)/shard_map/j,jxyz->xyz/dot_general | solution.py:196
  760.8 17.9 %all_to_all.93 = bf16[2,64,32,128]{3,2,0,1:T(8,128)(2,1)S(1)} all-to-all(bf16[2,64,32,128]{3,2,0,1:T(8,128)(2,1)} %reshape.2948), channel_id=1, replica_groups=mesh['band'=8,'grid'=4] {'grid'}, dimensions={1} | all-to-all | bytes 2097152 | tf_op jit(solution)/shard_map/all_to_all | solution.py:129
  780.0 3.9 reshape.2867
  788.0 16.9 %all_to_all.94 = bf16[2,16,128,128]{3,1,0,2:T(8,128)(2,1)S(1)} all-to-all(bf16[2,16,128,128]{3,1,0,2:T(8,128)(2,1)S(1)} %copy.101), channel_id=1, replica_groups=mesh['band'=8,'grid'=4] {'grid'}, dimensions={2} | all-to-all | bytes 2097152 | tf_op jit(solution)/shard_map/all_to_all | solution.py:139
  807.1 5.3 copy.105
  817.0 9.8 fusion.23
  826.8 4.8 fusion.22
  831.6 61.9 %all-reduce.23.cloned.1.call-done = bf16[32,128,128]{2,1,0:T(8,128)(2,1)} async-done(((bf16[32,128,128]{2,1,0:T(8,128)(2,1)}), bf16[32,128,128]{2,1,0:T(8,128)(2,1)}) %all-reduce.23.cloned.1.call-update) | async-done | bytes 1048592 | tf_op jit(solution)/shard_map/psum | solution.py:159
  893.5 4.0 fusion.186
  897.5 2.9 copy-done.1
  900.4 9.4 pad_maximum_fusion.4
  909.8 43.1 %fusion.107 = f32[6]{0:T(128)S(1)} fusion(f32[32,128,128,1]{2,3,1,0:T(1,128)S(1)} %bitcast.537, f32[6,32,128,128]{3,2,1,0:T(8,128)S(1)} %get-tuple-element.1321), kind=kOutput, calls=%fused_computation.126 | convolution fusion | flops 37748744 | bytes 14680088 | tf_op jit(solution)/shard_map/dot_general | solution.py:181
  952.9 42.9 %fusion.104 = f32[6]{0:T(128)S(1)} fusion(f32[32,128,128,1]{2,3,1,0:T(1,128)S(1)} %bitcast.536, f32[6,32,128,128]{3,2,1,0:T(8,128)S(1)} %get-tuple-element.1321), kind=kOutput, calls=%fused_computation.125 | convolution fusion | flops 37748744 | bytes 14680088 | tf_op jit(solution)/shard_map/dot_general | solution.py:179
  995.8 6.5 all-reduce.12
  1069.1 27.6 %fusion.12 = f32[1,32,128,128]{3,0,2,1:T(1,128)S(1)} fusion(f32[6,32,128,128]{3,2,1,0:T(8,128)} %get-tuple-element.1322, f32[6]{0:T(128)S(1)} %constant_dynamic-update-slice_fusion.24), kind=kOutput, calls=%fused_computation.20 | convolution fusion | flops 37748736 | bytes 14680088 | tf_op jit(solution)/shard_map/j,jxyz->xyz/dot_general | solution.py:196
  (321 shorter events, 131.2 us)
Async XLA Ops:
  7.6 4.2 copy-start.10
  7.6 4.2 copy-start.15
  24.1 18.7 %all-to-all-start = ((bf16[2,64,32,128]{3,2,0,1:T(8,128)(2,1)}), bf16[2,64,32,128]{3,2,0,1:T(8,128)(2,1)S(1)}, u32[]{:S(2)}, u32[]{:S(2)}) async-start(bf16[2,64,32,128]{3,2,0,1:T(8,128)(2,1)} %reshape.2946), calls=%async_computation | async-start | bytes 2097152 | tf_op jit(solution)/shard_map/all_to_all | solution.py:129
  28.3 147.9 %all-reduce.19.cloned.1.call-start = ((), (), s32[]{:S(2)}) async-start(), calls=%async_computation.6 | async-start | bytes 2097152 | tf_op jit(solution)/shard_map/psum | solution.py:159
  92.2 1.3 copy-start.21
  93.6 1.9 copy-start.4
  96.7 447.1 %all-reduce.21.cloned.1.call-start = ((), (), s32[]{:S(2)}) async-start(), calls=%async_computation.7 | async-start | bytes 2097152 | tf_op jit(solution)/shard_map/psum | solution.py:159
  180.1 13.4 %copy-start.14 = (f32[1,32,128,128]{3,2,1,0:T(8,128)}, f32[1,32,128,128]{3,2,1,0:T(8,128)S(1)}, u32[]{:S(2)}) copy-start(f32[1,32,128,128]{3,2,1,0:T(8,128)S(1)} %get-tuple-element.1331) | copy-start | bytes 6291460
  180.1 13.4 %copy-start.7 = (f32[32,128,128]{2,1,0:T(8,128)}, f32[32,128,128]{2,1,0:T(8,128)S(1)}, u32[]{:S(2)}) copy-start(f32[32,128,128]{2,1,0:T(8,128)S(1)} %get-tuple-element.1320) | copy-start | bytes 6291460
  353.0 28.1 %copy-start.8 = (f32[32,128,128]{2,1,0:T(8,128)S(1)}, f32[32,128,128]{2,1,0:T(8,128)}, u32[]{:S(2)}) copy-start(f32[32,128,128]{2,1,0:T(8,128)} %copy-done.7) | copy-start | bytes 6291460
  353.0 28.1 %copy-start.11 = (f32[32,128,128]{2,1,0:T(8,128)S(1)}, f32[32,128,128]{2,1,0:T(8,128)}, u32[]{:S(2)}) copy-start(f32[32,128,128]{2,1,0:T(8,128)} %param.227) | copy-start | bytes 6291460
  353.1 28.1 %copy-start.16 = (f32[32,128,128]{2,1,0:T(8,128)S(1)}, f32[32,128,128]{2,1,0:T(8,128)}, u32[]{:S(2)}) copy-start(f32[32,128,128]{2,1,0:T(8,128)} %param.226) | copy-start | bytes 6291460
  383.6 2.2 copy-start.5
  464.1 2.0 copy-start.2
  467.4 426.1 %all-reduce.23.cloned.1.call-start = ((), (), s32[]{:S(2)}) async-start(), calls=%async_computation.8 | async-start | bytes 2097152 | tf_op jit(solution)/shard_map/psum | solution.py:159
  543.8 8.4 copy-start
  547.8 13.7 %copy-start.19 = (f32[1,32,128,128]{3,2,1,0:T(8,128)}, f32[1,32,128,128]{3,2,1,0:T(8,128)S(1)}, u32[]{:S(2)}) copy-start(f32[1,32,128,128]{3,2,1,0:T(8,128)S(1)} %get-tuple-element.1330) | copy-start | bytes 6291460
  547.8 56.7 %copy-start.9 = (f32[32,128,128]{2,1,0:T(8,128)}, f32[32,128,128]{2,1,0:T(8,128)S(1)}, u32[]{:S(2)}) copy-start(f32[32,128,128]{2,1,0:T(8,128)S(1)} %get-tuple-element.1315) | copy-start | bytes 6291460
  547.9 201.5 %copy-start.6 = (f32[32,128,128]{2,1,0:T(8,128)}, f32[32,128,128]{2,1,0:T(8,128)S(1)}, u32[]{:S(2)}) copy-start(f32[32,128,128]{2,1,0:T(8,128)S(1)} %get-tuple-element.1316) | copy-start | bytes 6291460
  721.2 28.1 %copy-start.12 = (f32[32,128,128]{2,1,0:T(8,128)S(1)}, f32[32,128,128]{2,1,0:T(8,128)}, u32[]{:S(2)}) copy-start(f32[32,128,128]{2,1,0:T(8,128)} %get-tuple-element.1318) | copy-start | bytes 6291460
  721.2 28.1 %copy-start.17 = (f32[32,128,128]{2,1,0:T(8,128)S(1)}, f32[32,128,128]{2,1,0:T(8,128)}, u32[]{:S(2)}) copy-start(f32[32,128,128]{2,1,0:T(8,128)} %param.226) | copy-start | bytes 6291460
  751.8 2.2 copy-start.3
  815.6 11.2 %slice-start = ((s8[10485760]{0:T(1024)(128)(4,1)}), s8[2097152]{0:T(1024)(128)(4,1)S(1)}, s32[]{:S(2)}) async-start(s8[10485760]{0:T(1024)(128)(4,1)} %bitcast.525), calls=%async_computation.9 | async-start | bytes 4194304
  817.0 9.8 slice-start.1
  817.0 9.8 slice-start.2
  817.0 9.8 copy-start.20
  893.5 6.9 copy-start.1
  897.5 199.2 %copy-start.13 = (f32[32,128,128]{2,1,0:T(8,128)}, f32[32,128,128]{2,1,0:T(8,128)S(1)}, u32[]{:S(2)}) copy-start(f32[32,128,128]{2,1,0:T(8,128)S(1)} %get-tuple-element.1312) | copy-start | bytes 6291460
  1069.1 27.7 %copy-start.18 = (f32[32,128,128]{2,1,0:T(8,128)S(1)}, f32[32,128,128]{2,1,0:T(8,128)}, u32[]{:S(2)}) copy-start(f32[32,128,128]{2,1,0:T(8,128)} %get-tuple-element.1314) | copy-start | bytes 6291460
Sparse Core Ops, SparseCore 0:
  96.9 79.3 all-reduce.18
  467.5 76.2 all-reduce.20
  817.0 76.4 all-reduce.22
where the time goes:
time: 1120 us; the launch traced here: 1110 us
  matrix products  423 us (38%)
  waiting for transfers between devices  162 us (14%)
  between operations  152 us (14%)
  other arithmetic  126 us (11%)
  local copies, waits for them, and re-layouts  119 us (11%)
  blocking collectives  119 us (11%)
    psum x3, waiting for transfers between devices, local(): lax.psum((jnp.sum(weighted_sq, axis=0) * (density_scale / bands_total)).a...  148 us
    dot_general x3, matrix products, local(): jnp.dot(flat_diffs, mixing_residual.reshape(-1), precision=highest)  129 us
    dot_general x3, matrix products, local(): jnp.dot(flat_diffs, newest.reshape(-1), precision=highest) / cells_total  129 us
    dot_general x3, matrix products, local(): jnp.einsum('j,jxyz->xyz', coeffs, combined, precision=highest)  83.8 us
    all_to_all x3, blocking collectives, local(): lax.all_to_all(spatial.astype(jnp.bfloat16).reshape(item_count, column_ro...  63.3 us
    dot_general x1, matrix products, local(): jnp.dot(history_flat, history_flat.T, precision=highest) / cells_total  54.3 us
    concatenate x4, other arithmetic, local(): jnp.concatenate([mixing_residual_diffs[mixing_residual_diffs.shape[0] - (...  41.9 us
    all_to_all x2, blocking collectives, local(): lax.all_to_all(along_y, 'grid', split_axis=1, concat_axis=2, tiled=True)  35.8 us
  transfers between devices with their start and end apart: 4, of which 4 were waited for; matrix products, arithmetic and copies ran while one was open for 8% of the time, Pallas kernels for 0%

commit v1 on v0

--- a/solution.py
+++ b/solution.py
@@ -156,9 +156,12 @@
         weighted_sq = occupations[:, None, None, None] * (
             real_part * real_part + imag_part * imag_part
         )
-        density_out = lax.psum(
-            (jnp.sum(weighted_sq, axis=0) * (density_scale / bands_total)).astype(jnp.bfloat16),
-            "band",
+        density_out = jnp.sum(
+            lax.all_gather(
+                (jnp.sum(weighted_sq, axis=0) * (density_scale / bands_total)).astype(jnp.bfloat16),
+                "band",
+            ),
+            axis=0,
         ).astype(jnp.float32)
         mixing_density_diffs = density_diffs
         mixing_residual_diffs = residual_diffs

time: 1120 us -> 1270 us (1.13)
  waiting for transfers between devices: 162 us -> 300 us
  other arithmetic: 126 us -> 150 us
    all_gather x0 -> x3, waiting for transfers between devices: none -> 287 us  [local(): lax.all_gather((jnp.sum(weighted_sq, axis=0) * (density_scale / bands_tot...]
    psum x3 -> x0, waiting for transfers between devices: 148 us -> none  [local(): lax.psum((jnp.sum(weighted_sq, axis=0) * (density_scale / bands_total)).a...]
    reduce_sum x0 -> x3, other arithmetic: none -> 18.1 us  [local(): jnp.sum(lax.all_gather((jnp.sum(weighted_sq, axis=0) * (density_scale / b...]
  transfers between devices with their start and end apart: 4 -> 4, of which waited for: 4 -> 4; matrix products, arithmetic and copies ran while one was open for 8% -> 7% of each run, Pallas kernels for 0% -> 0%
where the time goes in v1:
time: 1270 us; the launch traced here: 1260 us
  matrix products  424 us (33%)
  waiting for transfers between devices  300 us (24%)
  between operations  152 us (12%)
  other arithmetic  150 us (12%)
  blocking collectives  118 us (9%)
  local copies, waits for them, and re-layouts  114 us (9%)
    all_gather x3, waiting for transfers between devices, local(): lax.all_gather((jnp.sum(weighted_sq, axis=0) * (density_scale / bands_tot...  287 us
    dot_general x3, matrix products, local(): jnp.dot(flat_diffs, mixing_residual.reshape(-1), precision=highest)  129 us
    dot_general x3, matrix products, local(): jnp.dot(flat_diffs, newest.reshape(-1), precision=highest) / cells_total  129 us
    dot_general x3, matrix products, local(): jnp.einsum('j,jxyz->xyz', coeffs, combined, precision=highest)  83.9 us
    all_to_all x3, blocking collectives, local(): lax.all_to_all(spatial.astype(jnp.bfloat16).reshape(item_count, column_ro...  64.9 us
    dot_general x1, matrix products, local(): jnp.dot(history_flat, history_flat.T, precision=highest) / cells_total  54.3 us
    concatenate x4, other arithmetic, local(): jnp.concatenate([mixing_residual_diffs[mixing_residual_diffs.shape[0] - (...  47.4 us
    all_to_all x2, blocking collectives, local(): lax.all_to_all(along_y, 'grid', split_axis=1, concat_axis=2, tiled=True)  35.8 us
  transfers between devices with their start and end apart: 4, of which 4 were waited for; matrix products, arithmetic and copies ran while one was open for 7% of the time, Pallas kernels for 0%

profile of v1, /device:TPU:0, one launch (start us, length us, event | category | flops | bytes accessed | tf_op | source)
XLA Modules:
  0.0 1262.6 jit_solution(14116712945984652795)
XLA Ops:
  7.6 4.1 slice_bitcast_fusion.1
  14.5 4.4 fusion.49
  24.1 4.2 all-to-all-start
  29.3 13.4 %all-to-all-done = bf16[2,64,32,128]{3,2,0,1:T(8,128)(2,1)S(1)} async-done(((bf16[2,64,32,128]{3,2,0,1:T(8,128)(2,1)}), bf16[2,64,32,128]{3,2,0,1:T(8,128)(2,1)S(1)}, u32[]{:S(2)}, u32[]{:S(2)}) %all-to-all-start) | async-done | bytes 1048608 | tf_op jit(solution)/shard_map/all_to_all | solution.py:129
  43.9 3.9 reshape.2858
  51.8 29.7 %all_to_all.90 = bf16[2,16,128,128]{3,1,0,2:T(8,128)(2,1)S(1)} all-to-all(bf16[2,16,128,128]{3,1,0,2:T(8,128)(2,1)S(1)} %copy.65), channel_id=1, replica_groups=mesh['band'=8,'grid'=4] {'grid'}, dimensions={2} | all-to-all | bytes 2097152 | tf_op jit(solution)/shard_map/all_to_all | solution.py:139
  82.9 3.9 reshape.2860
  86.7 4.3 copy.69
  98.1 54.3 %fusion.83 = f32[5,5]{1,0:T(8,128)S(1)} fusion(f32[5,32,128,128]{3,2,1,0:T(8,128)} %param.231), kind=kOutput, calls=%fused_computation.118 | convolution fusion | flops 157286432 | bytes 10485860 | tf_op jit(solution)/shard_map/dot_general | solution.py:105
  152.4 71.4 %all-gather.7.cloned.1.call-done = bf16[256,128,128]{2,1,0:T(8,128)(2,1)} async-done(((bf16[32,128,128]{2,1,0:T(8,128)(2,1)}), bf16[256,128,128]{2,1,0:T(8,128)(2,1)}) %all-gather.7.cloned.1.call-update) | async-done | bytes 8388624 | tf_op jit(solution)/shard_map/all_gather | solution.py:160
  223.8 6.4 reduce_sum.662
  230.2 3.9 fusion.188
  234.0 13.4 %pad_maximum_fusion = (f32[6,32,128,128]{3,2,1,0:T(8,128)S(1)}, f32[6,32,128,128]{3,2,1,0:T(8,128)}) fusion(f32[1,32,128,128]{3,2,1,0:T(8,128)S(1)} %bitcast.530, f32[5,32,128,128]{3,2,1,0:T(8,128)} %param.231, f32[1,32,128,128]{3,2,1,0:T(8,128)S(1)} %get-tuple-element.1331, f32[5,32,128,128]{3,2,1,0:T(8,128)} %param.230), kind=kLoop, calls=%fused_computation.13 | loop fusion | flops 12582912 | bytes 50331648 | tf_op jit(solution)/shard_map/concatenate | solution.py:177
  247.5 43.1 %fusion.119 = f32[6]{0:T(128)S(1)} fusion(f32[32,128,128,1]{2,3,1,0:T(1,128)S(1)} %bitcast.534, f32[6,32,128,128]{3,2,1,0:T(8,128)S(1)} %get-tuple-element.1325), kind=kOutput, calls=%fused_computation.130 | convolution fusion | flops 37748744 | bytes 14680088 | tf_op jit(solution)/shard_map/dot_general | solution.py:184
  290.5 42.8 %fusion.116 = f32[6]{0:T(128)S(1)} fusion(f32[32,128,128,1]{2,3,1,0:T(1,128)S(1)} %bitcast.531, f32[6,32,128,128]{3,2,1,0:T(8,128)S(1)} %get-tuple-element.1325), kind=kOutput, calls=%fused_computation.129 | convolution fusion | flops 37748744 | bytes 14680088 | tf_op jit(solution)/shard_map/dot_general | solution.py:182
  333.4 5.9 all-reduce.14
  406.0 28.1 %fusion.16 = f32[1,32,128,128]{3,0,2,1:T(1,128)S(1)} fusion(f32[6,32,128,128]{3,2,1,0:T(8,128)} %get-tuple-element.1326, f32[6]{0:T(128)S(1)} %constant_dynamic-update-slice_fusion.26), kind=kOutput, calls=%fused_computation.24 | convolution fusion | flops 37748736 | bytes 14680088 | tf_op jit(solution)/shard_map/j,jxyz->xyz/dot_general | solution.py:199
  441.5 3.5 copy.190
  445.1 4.7 reshape.2989
  449.8 17.9 %all_to_all.91 = bf16[2,64,32,128]{3,2,0,1:T(8,128)(2,1)S(1)} all-to-all(bf16[2,64,32,128]{3,2,0,1:T(8,128)(2,1)} %reshape.2989), channel_id=1, replica_groups=mesh['band'=8,'grid'=4] {'grid'}, dimensions={1} | all-to-all | bytes 2097152 | tf_op jit(solution)/shard_map/all_to_all | solution.py:129
  468.8 5.0 reshape.2882
  473.9 3.4 fusion.78
  482.2 18.1 %all_to_all.92 = bf16[2,16,128,128]{3,1,0,2:T(8,128)(2,1)S(1)} all-to-all(bf16[2,16,128,128]{3,1,0,2:T(8,128)(2,1)} %copy.84), channel_id=1, replica_groups=mesh['band'=8,'grid'=4] {'grid'}, dimensions={2} | all-to-all | bytes 2097152 | tf_op jit(solution)/shard_map/all_to_all | solution.py:139
  501.7 5.0 reshape.2884
  506.7 6.5 copy.88
  520.5 15.1 %fusion.24 = (f32[5,32,128,128]{3,2,1,0:T(8,128)}, f32[5,32,128,128]{3,2,1,0:T(8,128)}) fusion(f32[5,32,128,128]{3,2,1,0:T(8,128)} %param.230, f32[1,32,128,128]{3,2,1,0:T(8,128)} %copy-done.15, f32[1,32,128,128]{3,2,1,0:T(8,128)S(1)} %bitcast.532, f32[5,32,128,128]{3,2,1,0:T(8,128)} %param.231), kind=kLoop, calls=%fused_computation.38 | loop fusion | flops 5242880 | bytes 46137344 | tf_op jit(solution)/shard_map/concatenate | solution.py:170
  535.6 107.6 %all-gather.9.cloned.1.call-done = bf16[256,128,128]{2,1,0:T(8,128)(2,1)} async-done(((bf16[32,128,128]{2,1,0:T(8,128)(2,1)}), bf16[256,128,128]{2,1,0:T(8,128)(2,1)}) %all-gather.9.cloned.1.call-update) | async-done | bytes 8388624 | tf_op jit(solution)/shard_map/all_gather | solution.py:160
  643.2 6.4 reduce_sum.684
  649.6 3.9 fusion.187
  653.5 14.1 %pad_maximum_fusion.2 = (f32[6,32,128,128]{3,2,1,0:T(8,128)S(1)}, f32[6,32,128,128]{3,2,1,0:T(8,128)}) fusion(f32[1,32,128,128]{3,2,1,0:T(8,128)S(1)} %bitcast.535, f32[5,32,128,128]{3,2,1,0:T(8,128)} %get-tuple-element.1472, f32[1,32,128,128]{3,2,1,0:T(8,128)S(1)} %get-tuple-element.1330, f32[5,32,128,128]{3,2,1,0:T(8,128)} %get-tuple-element.1471), kind=kLoop, calls=%fused_computation.17 | loop fusion | flops 12582912 | bytes 50331648 | tf_op jit(solution)/shard_map/concatenate | solution.py:177
  667.5 43.1 %fusion.113 = f32[6]{0:T(128)S(1)} fusion(f32[32,128,128,1]{2,3,1,0:T(1,128)S(1)} %bitcast.533, f32[6,32,128,128]{3,2,1,0:T(8,128)S(1)} %get-tuple-element.1323), kind=kOutput, calls=%fused_computation.128 | convolution fusion | flops 37748744 | bytes 14680088 | tf_op jit(solution)/shard_map/dot_general | solution.py:184
  710.7 42.9 %fusion.110 = f32[6]{0:T(128)S(1)} fusion(f32[32,128,128,1]{2,3,1,0:T(1,128)S(1)} %bitcast.536, f32[6,32,128,128]{3,2,1,0:T(8,128)S(1)} %get-tuple-element.1323), kind=kOutput, calls=%fused_computation.127 | convolution fusion | flops 37748744 | bytes 14680088 | tf_op jit(solution)/shard_map/dot_general | solution.py:182
  753.5 5.8 all-reduce.13
  826.7 28.1 %fusion.14 = f32[1,32,128,128]{3,0,2,1:T(1,128)S(1)} fusion(f32[6,32,128,128]{3,2,1,0:T(8,128)} %get-tuple-element.1324, f32[6]{0:T(128)S(1)} %constant_dynamic-update-slice_fusion.25), kind=kOutput, calls=%fused_computation.22 | convolution fusion | flops 37748736 | bytes 14680088 | tf_op jit(solution)/shard_map/j,jxyz->xyz/dot_general | solution.py:199
  866.3 17.9 %all_to_all.93 = bf16[2,64,32,128]{3,2,0,1:T(8,128)(2,1)S(1)} all-to-all(bf16[2,64,32,128]{3,2,0,1:T(8,128)(2,1)} %reshape.2990), channel_id=1, replica_groups=mesh['band'=8,'grid'=4] {'grid'}, dimensions={1} | all-to-all | bytes 2097152 | tf_op jit(solution)/shard_map/all_to_all | solution.py:129
  885.4 3.9 reshape.2906
  893.5 17.1 %all_to_all.94 = bf16[2,16,128,128]{3,1,0,2:T(8,128)(2,1)S(1)} all-to-all(bf16[2,16,128,128]{3,1,0,2:T(8,128)(2,1)S(1)} %copy.101), channel_id=1, replica_groups=mesh['band'=8,'grid'=4] {'grid'}, dimensions={2} | all-to-all | bytes 2097152 | tf_op jit(solution)/shard_map/all_to_all | solution.py:139
  912.8 5.3 copy.105
  922.7 10.1 fusion.23
  932.9 4.8 fusion.22
  937.7 107.7 %all-gather.11.cloned.1.call-done = bf16[256,128,128]{2,1,0:T(8,128)(2,1)} async-done(((bf16[32,128,128]{2,1,0:T(8,128)(2,1)}), bf16[256,128,128]{2,1,0:T(8,128)(2,1)}) %all-gather.11.cloned.1.call-update) | async-done | bytes 8388624 | tf_op jit(solution)/shard_map/all_gather | solution.py:160
  1045.4 5.4 reduce_sum.706
  1050.8 4.4 fusion.186
  1057.6 9.8 pad_maximum_fusion.4
  1067.4 43.1 %fusion.107 = f32[6]{0:T(128)S(1)} fusion(f32[32,128,128,1]{2,3,1,0:T(1,128)S(1)} %bitcast.540, f32[6,32,128,128]{3,2,1,0:T(8,128)S(1)} %get-tuple-element.1321), kind=kOutput, calls=%fused_computation.126 | convolution fusion | flops 37748744 | bytes 14680088 | tf_op jit(solution)/shard_map/dot_general | solution.py:184
  1110.5 42.9 %fusion.104 = f32[6]{0:T(128)S(1)} fusion(f32[32,128,128,1]{2,3,1,0:T(1,128)S(1)} %bitcast.539, f32[6,32,128,128]{3,2,1,0:T(8,128)S(1)} %get-tuple-element.1321), kind=kOutput, calls=%fused_computation.125 | convolution fusion | flops 37748744 | bytes 14680088 | tf_op jit(solution)/shard_map/dot_general | solution.py:182
  1153.4 5.8 all-reduce.12
  1226.1 27.7 %fusion.12 = f32[1,32,128,128]{3,0,2,1:T(1,128)S(1)} fusion(f32[6,32,128,128]{3,2,1,0:T(8,128)} %get-tuple-element.1322, f32[6]{0:T(128)S(1)} %constant_dynamic-update-slice_fusion.24), kind=kOutput, calls=%fused_computation.20 | convolution fusion | flops 37748736 | bytes 14680088 | tf_op jit(solution)/shard_map/j,jxyz->xyz/dot_general | solution.py:199
  (326 shorter events, 136.3 us)
Async XLA Ops:
  7.6 4.2 copy-start.10
  7.6 4.2 copy-start.16
  24.1 18.7 %all-to-all-start = ((bf16[2,64,32,128]{3,2,0,1:T(8,128)(2,1)}), bf16[2,64,32,128]{3,2,0,1:T(8,128)(2,1)S(1)}, u32[]{:S(2)}, u32[]{:S(2)}) async-start(bf16[2,64,32,128]{3,2,0,1:T(8,128)(2,1)} %reshape.2988), calls=%async_computation | async-start | bytes 2097152 | tf_op jit(solution)/shard_map/all_to_all | solution.py:129
  28.3 195.4 %all-gather.7.cloned.1.call-start = ((), (), s32[]{:S(2)}) async-start(), calls=%async_computation.6 | async-start | bytes 9437184 | tf_op jit(solution)/shard_map/all_gather | solution.py:160
  93.6 1.3 copy-start.22
  94.9 1.9 copy-start.3
  98.1 545.1 %all-gather.9.cloned.1.call-start = ((), (), s32[]{:S(2)}) async-start(), calls=%async_computation.7 | async-start | bytes 9437184 | tf_op jit(solution)/shard_map/all_gather | solution.py:160
  234.0 13.4 %copy-start.15 = (f32[1,32,128,128]{3,2,1,0:T(8,128)}, f32[1,32,128,128]{3,2,1,0:T(8,128)S(1)}, u32[]{:S(2)}) copy-start(f32[1,32,128,128]{3,2,1,0:T(8,128)S(1)} %get-tuple-element.1331) | copy-start | bytes 6291460
  234.0 13.4 %copy-start.7 = (f32[32,128,128]{2,1,0:T(8,128)}, f32[32,128,128]{2,1,0:T(8,128)S(1)}, u32[]{:S(2)}) copy-start(f32[32,128,128]{2,1,0:T(8,128)S(1)} %get-tuple-element.1320) | copy-start | bytes 6291460
  406.0 28.1 %copy-start.8 = (f32[32,128,128]{2,1,0:T(8,128)S(1)}, f32[32,128,128]{2,1,0:T(8,128)}, u32[]{:S(2)}) copy-start(f32[32,128,128]{2,1,0:T(8,128)} %copy-done.7) | copy-start | bytes 6291460
  406.0 28.1 %copy-start.11 = (f32[32,128,128]{2,1,0:T(8,128)S(1)}, f32[32,128,128]{2,1,0:T(8,128)}, u32[]{:S(2)}) copy-start(f32[32,128,128]{2,1,0:T(8,128)} %param.227) | copy-start | bytes 6291460
  406.0 28.1 %copy-start.17 = (f32[32,128,128]{2,1,0:T(8,128)S(1)}, f32[32,128,128]{2,1,0:T(8,128)}, u32[]{:S(2)}) copy-start(f32[32,128,128]{2,1,0:T(8,128)} %param.226) | copy-start | bytes 6291460
  436.5 2.2 copy-start.4
  517.1 2.0 copy-start.1
  520.4 525.1 %all-gather.11.cloned.1.call-start = ((), (), s32[]{:S(2)}) async-start(), calls=%async_computation.8 | async-start | bytes 9437184 | tf_op jit(solution)/shard_map/all_gather | solution.py:160
  653.4 14.1 %copy-start.20 = (f32[1,32,128,128]{3,2,1,0:T(8,128)}, f32[1,32,128,128]{3,2,1,0:T(8,128)S(1)}, u32[]{:S(2)}) copy-start(f32[1,32,128,128]{3,2,1,0:T(8,128)S(1)} %get-tuple-element.1330) | copy-start | bytes 6291460
  653.4 57.2 %copy-start.9 = (f32[32,128,128]{2,1,0:T(8,128)}, f32[32,128,128]{2,1,0:T(8,128)S(1)}, u32[]{:S(2)}) copy-start(f32[32,128,128]{2,1,0:T(8,128)S(1)} %get-tuple-element.1315) | copy-start | bytes 6291460
  653.5 201.4 %copy-start.5 = (f32[32,128,128]{2,1,0:T(8,128)}, f32[32,128,128]{2,1,0:T(8,128)S(1)}, u32[]{:S(2)}) copy-start(f32[32,128,128]{2,1,0:T(8,128)S(1)} %get-tuple-element.1316) | copy-start | bytes 6291460
  826.7 28.1 %copy-start.12 = (f32[32,128,128]{2,1,0:T(8,128)S(1)}, f32[32,128,128]{2,1,0:T(8,128)}, u32[]{:S(2)}) copy-start(f32[32,128,128]{2,1,0:T(8,128)} %get-tuple-element.1318) | copy-start | bytes 6291460
  826.7 28.1 %copy-start.18 = (f32[32,128,128]{2,1,0:T(8,128)S(1)}, f32[32,128,128]{2,1,0:T(8,128)}, u32[]{:S(2)}) copy-start(f32[32,128,128]{2,1,0:T(8,128)} %param.226) | copy-start | bytes 6291460
  857.3 2.2 copy-start.2
  921.3 11.6 slice-start
  922.7 10.1 slice-start.1
  922.7 10.1 slice-start.2
  922.7 10.2 copy-start.21
  1045.4 5.4 copy-start.6
  1050.8 6.8 copy-start
  1055.2 12.2 copy-start.13
  1226.1 27.7 %copy-start.14 = (f32[32,128,128]{2,1,0:T(8,128)S(1)}, f32[32,128,128]{2,1,0:T(8,128)}, u32[]{:S(2)}) copy-start(f32[32,128,128]{2,1,0:T(8,128)} %copy-done.13) | copy-start | bytes 6291460
  1226.1 27.7 %copy-start.19 = (f32[32,128,128]{2,1,0:T(8,128)S(1)}, f32[32,128,128]{2,1,0:T(8,128)}, u32[]{:S(2)}) copy-start(f32[32,128,128]{2,1,0:T(8,128)} %get-tuple-element.1314) | copy-start | bytes 6291460
Sparse Core Ops, SparseCore 0:
  98.2 125.5 all-gather.6
  520.5 122.6 all-gather.8
  922.8 122.6 all-gather.10
